TPU v7x, 32 devices: a whole 2x2x4 slice. The times are simulated.
32 devices in a mesh: dp: 2 (over x), ctx: 16 (over z, y, core).
Axes of the slice: x: 2, y: 2, z: 4, core: 2. Of those that a mesh axis runs over, the one named last changes fastest.
Arguments:
- patches: bfloat16 [2, 1024, 1280], P('dp', 'ctx'), may hold values from -6 to 6
- vit_norm_gain: float32 [1280], replicated, may hold values from 0.1 to 1.9
- vit_qkv: bfloat16 [1280, 1920], P('dp'), may hold values from -0.15625 to 0.15625
- vit_out: bfloat16 [640, 1280], P('dp'), may hold values from -0.25 to 0.25
- merger: bfloat16 [5120, 8192], P('dp', 'ctx'), may hold values from -0.078125 to 0.078125
- text_embed: bfloat16 [2, 2048, 8192], P('dp', 'ctx'), may hold values from -6 to 6
- lang_norm_gain: float32 [8192], replicated, may hold values from 0.1 to 1.9
- key_weight: bfloat16 [8192, 512], P('dp'), may hold values from -0.0625 to 0.0625
- key_cotangent: bfloat16 [2, 2048, 512], P('dp', 'ctx'), may hold values from -6 to 6
- image_grid: int32 [2, 16, 2], P('dp'), may hold values from 1 to 16, as said below
- image_start: int32 [2, 16], P('dp'), may hold values from 0 to 2047, as said below
Outputs:
- key_rot: bfloat16 [2, 2048, 512], P('dp', 'ctx')
- merger_grad: float32 [5120, 8192], P('dp', 'ctx')
Inputs may be any that keep to these rules, and one draw needn't show every extreme that they name: `image_grid`: the image held by device c of ctx has a grid of rows by columns merged tokens with rows times columns at most 16, equal to 16 for some device of every sequence. Its 4 * rows * columns patches are the first rows of that device's patch block, each 2x2 merge window as 4 consecutive rows, windows in row-major order; the remaining rows are unused. `image_start`: the image occupies rows * columns consecutive positions from here. The range of 128 positions of each device along ctx holds exactly one image, wholly.
All inputs are finite; a program needn't handle non-finite values.
Results may differ from a plain program's by a relative error of at most 0.015.
Values may be sent and summed in bfloat16 or wider, within the bound.
No kernel may reach another device: no remote copies, remote signals or barrier semaphores. Data moves between devices by JAX's collectives and lax.ppermute only.
A program may use at most 128 MiB of HBM per device.

v0:
```python
import math
import jax
import jax.numpy as jnp
from jax import lax
from jax.sharding import PartitionSpec as P

VHD = 80
HD = 128
EPS = 1e-06
THETA = 1000000.0


def layer_norm(values):
    average = jnp.mean(values, axis=-1, keepdims=True)
    centered = values - average
    variance = jnp.mean(centered * centered, axis=-1, keepdims=True)
    return centered * lax.rsqrt(variance + EPS)


def vision_image(patch_rows, count, norm_gain, qkv_weight, out_weight):
    values = patch_rows.astype(jnp.float32)
    normed = (layer_norm(values) * norm_gain).astype(jnp.bfloat16)
    projected = jnp.dot(normed, qkv_weight, preferred_element_type=jnp.float32).astype(jnp.bfloat16)
    width = qkv_weight.shape[1] // 3
    head_count = width // VHD
    queries = projected[:, :width].reshape(-1, head_count, VHD)
    key_vecs = projected[:, width : 2 * width].reshape(-1, head_count, VHD)
    value_vecs = projected[:, 2 * width :].reshape(-1, head_count, VHD)
    scores = jnp.einsum(
        "qhd,khd->hqk", queries, key_vecs, preferred_element_type=jnp.float32
    ) / math.sqrt(VHD)
    alive_mask = (jnp.arange(values.shape[0], dtype=jnp.int32) < 4 * count).astype(jnp.float32)
    weights = jnp.exp(scores) * alive_mask[None, None, :]
    probability = (weights / jnp.sum(weights, axis=-1, keepdims=True)).astype(jnp.bfloat16)
    attended = jnp.einsum(
        "hqk,khd->qhd", probability, value_vecs, preferred_element_type=jnp.float32
    )
    attended = attended.reshape(values.shape[0], width).astype(jnp.bfloat16)
    vit_hidden = values + jnp.dot(attended, out_weight, preferred_element_type=jnp.float32)
    merged = layer_norm(vit_hidden).astype(jnp.bfloat16).reshape(-1, 4 * values.shape[1])
    keeping = jnp.arange(merged.shape[0], dtype=jnp.int32) < count
    return jnp.where(keeping[:, None], merged, jnp.zeros_like(merged))


def rope_tables(pos_t, pos_h, pos_w):
    half_dim = HD // 2
    freq_index = jnp.arange(half_dim, dtype=jnp.int32)
    inverse = THETA ** (-(2.0 * freq_index.astype(jnp.float32)) / HD)
    first_cut = HD // 8
    second_cut = first_cut + 3 * HD // 16
    chosen = jnp.where(
        freq_index[None, :] < first_cut,
        pos_t[:, None],
        jnp.where(freq_index[None, :] < second_cut, pos_h[:, None], pos_w[:, None]),
    )
    angles = chosen.astype(jnp.float32) * inverse[None, :]
    return (jnp.cos(angles), jnp.sin(angles))


def rotate(vectors, cosine, sines):
    half_dim = vectors.shape[-1] // 2
    first_half = vectors[..., :half_dim]
    second_half = vectors[..., half_dim:]
    cos_part = cosine[:, None, :]
    sin_part = sines[:, None, :]
    return jnp.concatenate(
        [
            first_half * cos_part - second_half * sin_part,
            second_half * cos_part + first_half * sin_part,
        ],
        axis=-1,
    )


def unrotate(vectors, cosine, sines):
    half_dim = vectors.shape[-1] // 2
    first_half = vectors[..., :half_dim]
    second_half = vectors[..., half_dim:]
    cos_part = cosine[:, None, :]
    sin_part = sines[:, None, :]
    return jnp.concatenate(
        [
            first_half * cos_part + second_half * sin_part,
            second_half * cos_part - first_half * sin_part,
        ],
        axis=-1,
    )


def norm_backward(rows, grad_rows, gain):
    values = rows.astype(jnp.float32)
    row_scale = lax.rsqrt(jnp.mean(values * values, axis=-1, keepdims=True) + EPS)
    weighted = grad_rows * gain
    return row_scale * weighted - values * row_scale**3 * jnp.mean(
        values * weighted, axis=-1, keepdims=True
    )


def on_device(
    patches,
    vit_norm_gain,
    vit_qkv,
    vit_out,
    merger,
    text_embed,
    lang_norm_gain,
    key_weight,
    key_cotangent,
    image_grid,
    image_start,
):
    tokens = text_embed.shape[1]
    groups = lax.axis_size("ctx")
    own_index = lax.axis_index("ctx")
    qkv_full, out_full, merger_rows = (
        lax.all_gather(vit_qkv, "dp", axis=0, tiled=True),
        lax.all_gather(vit_out, "dp", axis=0, tiled=True),
        lax.all_gather(merger, "dp", axis=0, tiled=True),
    )
    grid_sizes = image_grid[0]
    start_pos = image_start[0]
    grid_rows = grid_sizes[:, 0]
    grid_cols = grid_sizes[:, 1]
    counts = grid_rows * grid_cols
    own_count = lax.dynamic_index_in_dim(counts, own_index, 0, keepdims=False)
    merged = vision_image(patches[0], own_count, vit_norm_gain, qkv_full, out_full)
    capacity = merged.shape[0]
    merged_all = lax.all_gather(merged, "ctx", axis=0, tiled=True)
    embedded = jnp.dot(merged_all, merger_rows, preferred_element_type=jnp.float32).astype(
        jnp.bfloat16
    )
    blocks = embedded.reshape(groups, capacity, -1)
    target_range = start_pos // tokens
    routing = (target_range[None, :] == jnp.arange(groups, dtype=jnp.int32)[:, None]).astype(
        jnp.bfloat16
    )
    outgoing = jnp.einsum(
        "do,okc->dkc", routing, blocks, preferred_element_type=jnp.float32
    ).astype(jnp.bfloat16)
    arrived = lax.all_to_all(outgoing, "ctx", split_axis=0, concat_axis=2, tiled=True)[0]
    own_range = target_range == own_index
    image_first = jnp.sum(jnp.where(own_range, start_pos, 0))
    own_cols = jnp.sum(jnp.where(own_range, grid_cols, 0))
    image_count = jnp.sum(jnp.where(own_range, counts, 0))
    offset = image_first - own_index * tokens
    local_index = jnp.arange(tokens, dtype=jnp.int32)
    inner_index = local_index - offset
    image_mask = (inner_index >= 0) & (inner_index < image_count)
    slot_index = jnp.arange(capacity, dtype=jnp.int32)
    slot_alive = slot_index < image_count
    selector = (inner_index[:, None] == slot_index[None, :]) & slot_alive[None, :]
    placed = jnp.dot(
        selector.astype(jnp.bfloat16), arrived, preferred_element_type=jnp.float32
    ).astype(jnp.bfloat16)
    hidden = jnp.where(image_mask[:, None], placed, text_embed[0])
    hidden_float = hidden.astype(jnp.float32)
    row_scale = lax.rsqrt(jnp.mean(hidden_float * hidden_float, axis=-1, keepdims=True) + EPS)
    normed = (hidden_float * row_scale * lang_norm_gain).astype(jnp.bfloat16)
    pieces = lax.all_to_all(normed, "dp", split_axis=1, concat_axis=0, tiled=True)
    key_proj = lax.psum_scatter(
        jnp.dot(pieces, key_weight, preferred_element_type=jnp.float32).astype(jnp.bfloat16),
        "dp",
        scatter_dimension=0,
        tiled=True,
    ).astype(jnp.float32)
    global_index = own_index * tokens + local_index
    inner_safe = jnp.clip(inner_index, 0, capacity - 1)
    pos_t = jnp.where(image_mask, image_first, global_index)
    pos_h = jnp.where(image_mask, image_first + inner_safe // own_cols, global_index)
    pos_w = jnp.where(image_mask, image_first + inner_safe % own_cols, global_index)
    cosine, sines = rope_tables(pos_t, pos_h, pos_w)
    head_count = key_weight.shape[1] // HD
    rotated = (
        rotate(key_proj.reshape(tokens, head_count, HD), cosine, sines)
        .reshape(tokens, -1)
        .astype(jnp.bfloat16)
    )
    grad_key = unrotate(
        key_cotangent[0].astype(jnp.float32).reshape(tokens, head_count, HD), cosine, sines
    ).reshape(tokens, -1)
    grad_image_key = jnp.dot(
        selector.T.astype(jnp.float32), grad_key, precision=lax.Precision.HIGHEST
    ).astype(jnp.bfloat16)
    all_grads = lax.all_gather(grad_image_key, "dp", axis=0, tiled=True)
    partial_value = lax.dot_general(
        all_grads, key_weight, (((1,), (1,)), ((), ())), preferred_element_type=jnp.float32
    )
    grad_normed = lax.all_to_all(
        partial_value.astype(jnp.bfloat16), "dp", split_axis=0, concat_axis=1, tiled=True
    ).astype(partial_value.dtype)
    grad_hidden = norm_backward(arrived, grad_normed, lang_norm_gain)
    grad_embedded = jnp.where(slot_alive[:, None], grad_hidden, 0.0).astype(jnp.bfloat16)
    returned = lax.all_to_all(grad_embedded[None], "ctx", split_axis=2, concat_axis=0, tiled=True)
    grad_blocks = jnp.einsum(
        "do,dkc->okc", routing, returned, preferred_element_type=jnp.float32
    ).astype(jnp.bfloat16)
    grad_all = grad_blocks.reshape(groups * capacity, -1)
    merger_grad = lax.psum_scatter(
        lax.dot_general(
            merged_all, grad_all, (((0,), (0,)), ((), ())), preferred_element_type=jnp.float32
        ).astype(jnp.bfloat16),
        "dp",
        scatter_dimension=0,
        tiled=True,
    ).astype(jnp.float32)
    return (rotated[None], merger_grad)


def solution(mesh):
    return jax.shard_map(
        on_device,
        mesh=mesh,
        in_specs=(
            P("dp", "ctx", None),
            P(),
            P("dp", None),
            P("dp", None),
            P("dp", "ctx"),
            P("dp", "ctx", None),
            P(),
            P("dp", None),
            P("dp", "ctx", None),
            P("dp", None, None),
            P("dp", None),
        ),
        out_specs=(P("dp", "ctx", None), P("dp", "ctx")),
        check_vma=False,
    )
```

profile of v0, /device:TPU:0, one launch (start us, length us, event | category | flops | bytes accessed | tf_op | source)
XLA Modules:
  0.0 469.2 jit_solution(12247656343845873802)
XLA Ops:
  7.2 0.7 all-gather.5.cloned.1.call-update
  8.0 0.7 all-gather.7.cloned.1.call-update
  8.7 0.7 all-gather.11.cloned.1.call-update
  9.5 0.7 fusion.37
  10.2 0.6 dynamic_slice.4
  11.4 0.7 iota_compare_fusion.4
  12.2 0.2 fusion.8
  12.5 64.7 %all-gather.5.cloned.1.call-done = bf16[1280,1920]{1,0:T(8,128)(2,1)} async-done(((bf16[640,1920]{1,0:T(8,128)(2,1)}), bf16[1280,1920]{1,0:T(8,128)(2,1)}) %all-gather.5.cloned.1.call-update) | async-done | bytes 4915216 | tf_op jit(solution)/shard_map/all_gather | solution.py:116
  77.2 3.4 convolution_convert_fusion.3
  80.6 0.2 reshape.486
  80.8 0.2 reshape.487
  80.9 0.2 reshape.485
  81.1 0.2 fusion.3
  81.3 0.3 fusion.4
  81.7 0.1 convert_element_type.170
  81.8 24.8 %all-gather.7.cloned.1.call-done = bf16[640,1280]{1,0:T(8,128)(2,1)} async-done(((bf16[320,1280]{1,0:T(8,128)(2,1)}), bf16[640,1280]{1,0:T(8,128)(2,1)}) %all-gather.7.cloned.1.call-update) | async-done | bytes 1638416 | tf_op jit(solution)/shard_map/all_gather | solution.py:117
  106.7 1.9 fusion.49
  108.6 0.2 multiply_reduce_fusion.3
  109.0 0.8 broadcast_select_fusion
  109.8 67.0 %all-gather.11.cloned.1.call-done = bf16[5120,512]{1,0:T(8,128)(2,1)} async-done(((bf16[2560,512]{1,0:T(8,128)(2,1)}), bf16[5120,512]{1,0:T(8,128)(2,1)}) %all-gather.11.cloned.1.call-update) | async-done | bytes 5242896 | tf_op jit(solution)/shard_map/all_gather | solution.py:118
  176.8 45.8 %all-gather.9.cloned.1.call-done = bf16[256,5120]{1,0:T(8,128)(2,1)} async-done(((bf16[16,5120]{1,0:T(8,128)(2,1)}), bf16[256,5120]{1,0:T(8,128)(2,1)}) %all-gather.9.cloned.1.call-update) | async-done | bytes 2621456 | tf_op jit(solution)/shard_map/all_gather | solution.py:128
  222.6 4.8 %convolution_convert_fusion.7 = bf16[256,512]{1,0:T(8,128)(2,1)S(1)} fusion(bf16[256,5120]{1,0:T(8,128)(2,1)} %all-gather.9.cloned.1.call-done, bf16[5120,512]{1,0:T(8,128)(2,1)} %all-gather.11.cloned.1.call-done), kind=kOutput, calls=%fused_computation.13 | convolution fusion | flops 1342308352 | bytes 8126464 | tf_op jit(solution)/shard_map/dot_general | solution.py:129
  227.4 0.4 convolution_convert_fusion.6
  227.8 0.9 copy.48
  228.6 3.6 all-to-all-start
  234.8 0.6 iota_compare_fusion.5
  235.4 1.3 fusion.39
  236.7 1.4 add_select_fusion.1
  238.1 4.0 all-to-all-done
  242.2 0.9 multiply_reduce_fusion
  243.1 0.5 multiply_convert_fusion
  243.8 28.0 %all_to_all.65 = bf16[128,2,4096]{2,0,1:T(8,128)(2,1)S(1)} all-to-all(bf16[128,2,4096]{2,0,1:T(8,128)(2,1)S(1)} %bitcast.113), channel_id=1, replica_groups=mesh['dp'=2,'ctx'=16] {'dp'}, dimensions={1} | all-to-all | bytes 4194304 | tf_op jit(solution)/shard_map/all_to_all | solution.py:159
  271.8 2.0 convolution_convert_fusion.5
  274.0 0.3 fusion.24
  274.3 9.1 %reduce-scatter.3.cloned.1.call-done = bf16[128,512]{1,0:T(8,128)(2,1)} async-done(((bf16[256,512]{1,0:T(8,128)(2,1)}), bf16[128,512]{1,0:T(8,128)(2,1)}) %reduce-scatter.3.cloned.1.call-update) | async-done | bytes 131088 | tf_op jit(solution)/shard_map/reduce_scatter | solution.py:160
  283.4 1.0 reshape.495
  284.4 0.5 multiply_add_fusion
  284.8 0.2 pad_maximum_fusion
  285.0 0.3 convolution_convert_fusion.9
  285.3 4.4 all_gather.19
  289.7 4.2 convolution_convert_fusion.2
  294.0 3.4 all-to-all-start.2
  297.4 0.2 reduce-scatter.5.cloned.1.call-start
  297.6 0.2 bitcast_convert_fusion
  297.9 4.7 all-to-all-done.2
  302.6 0.4 copy.51
  303.0 0.5 reshape.499
  303.5 0.5 reshape.497
  303.9 0.3 multiply_reduce_fusion.2
  304.3 0.2 select_convert_fusion
  304.4 6.7 %copy.53 = bf16[1,16,8192]{1,0,2:T(2,128)(2,1)} copy(bf16[1,16,8192]{2,1,0:T(8,128)(2,1)S(1)} %select_convert_fusion) | data formatting | bytes 524288 | tf_op jit(solution)/shard_map/convert_element_type | solution.py:192
  311.1 0.5 broadcast.478
  311.6 45.2 %reduce.3 = bf16[8192,16]{1,0:T(8,128)(2,1)S(1)} reduce(bf16[8192,1,16]{2,1,0:T(2,128)(2,1)} %bitcast.110, bf16[]{:T(256)} %broadcast.478), dimensions={1}, to_apply=%bitcast.90.reduce_sub_computation | reduce | bytes 524290
  356.8 2.1 reshape.502
  359.0 15.4 %all_to_all.66 = bf16[16,2,4096]{2,1,0:T(2,128)(2,1)S(1)} all-to-all(bf16[16,2,4096]{2,1,0:T(2,128)(2,1)S(1)} %reshape.502), channel_id=1, replica_groups=mesh['dp'=2,'ctx'=16] {'ctx'}, dimensions={0} | all-to-all | bytes 524288 | tf_op jit(solution)/shard_map/all_to_all | solution.py:193
  374.4 7.6 %reshape.503 = bf16[8192,1,16]{2,1,0:T(2,128)(2,1)} reshape(bf16[16,2,4096]{2,1,0:T(2,128)(2,1)S(1)} %all_to_all.66) | data formatting | bytes 524288
  382.0 7.9 %copy.54 = bf16[1,16,8192]{2,1,0:T(8,128)(2,1)S(1)} copy(bf16[1,16,8192]{1,0,2:T(2,128)(2,1)} %bitcast.111) | data formatting | bytes 524288 | tf_op jit(solution)/shard_map/all_to_all | solution.py:193
  390.0 0.3 convolution_convert_fusion.4
  390.3 0.2 copy.55
  390.4 3.9 convolution_convert_fusion.1
  394.4 0.2 pad_maximum_fusion.1
  394.6 0.7 convert_element_type.180
  395.3 62.3 %reduce-scatter.5.cloned.1.call-done = bf16[2560,512]{1,0:T(8,128)(2,1)} async-done(((bf16[5120,512]{1,0:T(8,128)(2,1)}), bf16[2560,512]{1,0:T(8,128)(2,1)}) %reduce-scatter.5.cloned.1.call-update) | async-done | bytes 2621456 | tf_op jit(solution)/shard_map/reduce_scatter | solution.py:198
  457.6 4.8 %convert_element_type.196 = f32[2560,512]{1,0:T(8,128)} convert(bf16[2560,512]{1,0:T(8,128)(2,1)} %reduce-scatter.5.cloned.1.call-done) | non-fusion elementwise | flops 1310720 | bytes 7864320 | tf_op jit(solution)/shard_map/convert_element_type | solution.py:205
  (49 shorter events, 1.3 us)
Async XLA Ops:
  7.2 2.3 copy-start.7
  7.2 2.3 copy-start.8
  7.2 4.9 %copy-start.2 = (bf16[1,64,1280]{2,1,0:T(8,128)(2,1)S(1)}, bf16[1,64,1280]{2,1,0:T(8,128)(2,1)}, u32[]{:S(2)}) copy-start(bf16[1,64,1280]{2,1,0:T(8,128)(2,1)} %param.11) | copy-start | bytes 491524
  7.2 70.0 %copy-start.6 = (f32[1280]{0:T(1024)S(1)}, f32[1280]{0:T(1024)}, u32[]{:S(2)}) copy-start(f32[1280]{0:T(1024)} %param.12) | copy-start | bytes 15364
  7.2 70.0 %all-gather.5.cloned.1.call-start = ((), (), s32[]{:S(2)}) async-start(), calls=%async_computation.6 | async-start | bytes 7372800 | tf_op jit(solution)/shard_map/all_gather | solution.py:116
  7.9 98.7 %all-gather.7.cloned.1.call-start = ((), (), s32[]{:S(2)}) async-start(), calls=%async_computation.7 | async-start | bytes 2457600 | tf_op jit(solution)/shard_map/all_gather | solution.py:117
  8.7 168.1 %all-gather.11.cloned.1.call-start = ((), (), s32[]{:S(2)}) async-start(), calls=%async_computation.9 | async-start | bytes 7864320 | tf_op jit(solution)/shard_map/all_gather | solution.py:118
  9.4 213.2 %all-gather.9.cloned.1.call-start = ((), (), s32[]{:S(2)}) async-start(), calls=%async_computation.8 | async-start | bytes 2785280 | tf_op jit(solution)/shard_map/all_gather | solution.py:128
  109.8 132.4 %copy-start.3 = (bf16[1,128,8192]{2,1,0:T(8,128)(2,1)S(1)}, bf16[1,128,8192]{2,1,0:T(8,128)(2,1)}, u32[]{:S(2)}) copy-start(bf16[1,128,8192]{2,1,0:T(8,128)(2,1)} %param.16) | copy-start | bytes 6291460
  227.7 15.4 %copy-start.4 = (f32[8192]{0:T(1024)S(1)}, f32[8192]{0:T(1024)}, u32[]{:S(2)}) copy-start(f32[8192]{0:T(1024)} %param.17) | copy-start | bytes 98308
  228.6 13.6 %all-to-all-start = ((bf16[16,16,512]{2,1,0:T(8,128)(2,1)}), bf16[16,16,512]{2,1,0:T(8,128)(2,1)S(1)}, u32[]{:S(2)}, u32[]{:S(2)}) async-start(bf16[16,16,512]{2,1,0:T(8,128)(2,1)} %copy.48), calls=%async_computation | async-start | bytes 524288 | tf_op jit(solution)/shard_map/all_to_all | solution.py:140
  232.2 51.2 %reduce-scatter.3.cloned.1.call-start = ((), (), s32[]{:S(2)}) async-start(), calls=%async_computation.10 | async-start | bytes 393216 | tf_op jit(solution)/shard_map/reduce_scatter | solution.py:160
  243.6 28.2 %copy-start.1 = (bf16[4096,512]{1,0:T(8,128)(2,1)S(1)}, bf16[4096,512]{1,0:T(8,128)(2,1)}, u32[]{:S(2)}) copy-start(bf16[4096,512]{1,0:T(8,128)(2,1)} %param.18) | copy-start | bytes 12582916
  271.8 2.1 copy-start.5
  294.0 8.6 %all-to-all-start.2 = ((bf16[2,16,4096]{2,1,0:T(8,128)(2,1)}), bf16[2,16,4096]{2,1,0:T(8,128)(2,1)S(1)}, u32[]{:S(2)}, u32[]{:S(2)}) async-start(bf16[2,16,4096]{2,1,0:T(8,128)(2,1)} %bitcast.17), calls=%async_computation.3 | async-start | bytes 524288 | tf_op jit(solution)/shard_map/all_to_all | solution.py:188
  297.4 160.2 %reduce-scatter.5.cloned.1.call-start = ((), (), s32[]{:S(2)}) async-start(), calls=%async_computation.11 | async-start | bytes 7864320 | tf_op jit(solution)/shard_map/reduce_scatter | solution.py:198
  374.4 16.0 %copy-start = (bf16[256,5120]{1,0:T(8,128)(2,1)S(1)}, bf16[256,5120]{1,0:T(8,128)(2,1)}, u32[]{:S(2)}) copy-start(bf16[256,5120]{1,0:T(8,128)(2,1)} %all-gather.9.cloned.1.call-done) | copy-start | bytes 7864324
Sparse Core Ops, SparseCore 0:
  9.6 67.5 all-gather.4
  78.7 27.9 all-gather.6
  108.2 68.5 all-gather.10
  179.5 43.0 all-gather.8
  274.0 9.3 reduce-scatter.2
  394.5 63.0 reduce-scatter.4
where the time goes:
time: 470 us; the launch traced here: 469 us
  waiting for transfers between devices  284 us (60%)
  other arithmetic  58.6 us (12%)
  blocking collectives  47.8 us (10%)
  local copies, waits for them, and re-layouts  30.7 us (7%)
  matrix products  22.5 us (5%)
  between operations  17.8 us (4%)
  starting transfers between devices  7.42 us (2%)
    all_gather x1, waiting for transfers between devices, on_device(): lax.all_gather(merger, 'dp', axis=0, tiled=True)  67 us
    all_gather x1, waiting for transfers between devices, on_device(): lax.all_gather(vit_qkv, 'dp', axis=0, tiled=True)  64.7 us
    reduce_scatter x1, waiting for transfers between devices, on_device(): lax.psum_scatter(lax.dot_general(merged_all, grad_all, (((0,), (0,)), (()...  62.3 us
    all_gather x1, waiting for transfers between devices, on_device(): merged_all = lax.all_gather(merged, 'ctx', axis=0, tiled=True)  45.8 us
    unnamed x1, other arithmetic  45.2 us
    all_to_all x1, blocking collectives, on_device(): lax.all_to_all(normed, 'dp', split_axis=1, concat_axis=0, tiled=True)  28 us
    all_gather x1, waiting for transfers between devices, on_device(): lax.all_gather(vit_out, 'dp', axis=0, tiled=True)  24.8 us
    all_to_all x1, blocking collectives, on_device(): lax.all_to_all(grad_embedded[None], 'ctx', split_axis=2, concat_axis=0, t...  15.4 us
  transfers between devices with their start and end apart: 8, of which 8 were waited for; matrix products, arithmetic and copies ran while one was open for 3% of the time, Pallas kernels for 0%

commit v1 on v0

--- a/solution.py
+++ b/solution.py
@@ -125,7 +125,12 @@
     own_count = lax.dynamic_index_in_dim(counts, own_index, 0, keepdims=False)
     merged = vision_image(patches[0], own_count, vit_norm_gain, qkv_full, out_full)
     capacity = merged.shape[0]
-    merged_all = lax.all_gather(merged, "ctx", axis=0, tiled=True)
+    ring = [merged]
+    for hop in range(15):
+        ring.append(lax.ppermute(ring[-1], "ctx", [(dev, (dev + 1) % 16) for dev in range(16)]))
+    merged_all = jnp.roll(
+        jnp.concatenate(ring[::-1], axis=0), (lax.axis_index("ctx") + 1) * ring[0].shape[0], axis=0
+    )
     embedded = jnp.dot(merged_all, merger_rows, preferred_element_type=jnp.float32).astype(
         jnp.bfloat16
     )

time: 470 us -> 526 us (1.12)
  waiting for transfers between devices: 284 us -> 313 us
  local copies, waits for them, and re-layouts: 30.7 us -> 51 us
    ppermute x0 -> x15, waiting for transfers between devices: none -> 112 us  [on_device(): lax.ppermute(ring[-1], 'ctx', [(dev, (dev + 1) % 16) for dev in range(16)])]
    all_gather x1 -> x0, waiting for transfers between devices: 45.8 us -> none  [on_device(): merged_all = lax.all_gather(merged, 'ctx', axis=0, tiled=True)]
    all_gather x1, waiting for transfers between devices: 67 us -> 32.2 us  [on_device(): lax.all_gather(merger, 'dp', axis=0, tiled=True)]
    unnamed x23 -> x47, local copies, waits for them, and re-layouts: 10.4 us -> 30.7 us
    unnamed x1 -> x2, other arithmetic: 45.2 us -> 46 us
  transfers between devices with their start and end apart: 8 -> 22, of which waited for: 8 -> 22; matrix products, arithmetic and copies ran while one was open for 3% -> 7% of each run, Pallas kernels for 0% -> 0%
where the time goes in v1:
time: 526 us; the launch traced here: 525 us
  waiting for transfers between devices  313 us (60%)
  other arithmetic  62.1 us (12%)
  local copies, waits for them, and re-layouts  51 us (10%)
  blocking collectives  47.8 us (9%)
  matrix products  24.3 us (5%)
  between operations  17.5 us (3%)
  starting transfers between devices  9.53 us (2%)
    ppermute x15, waiting for transfers between devices, on_device(): lax.ppermute(ring[-1], 'ctx', [(dev, (dev + 1) % 16) for dev in range(16)])  112 us
    all_gather x1, waiting for transfers between devices, on_device(): lax.all_gather(vit_qkv, 'dp', axis=0, tiled=True)  62.8 us
    reduce_scatter x1, waiting for transfers between devices, on_device(): lax.psum_scatter(lax.dot_general(merged_all, grad_all, (((0,), (0,)), (()...  62.3 us
    unnamed x2, other arithmetic  46 us
    all_gather x1, waiting for transfers between devices, on_device(): lax.all_gather(merger, 'dp', axis=0, tiled=True)  32.2 us
    unnamed x47, local copies, waits for them, and re-layouts  30.7 us
    all_to_all x1, blocking collectives, on_device(): lax.all_to_all(normed, 'dp', split_axis=1, concat_axis=0, tiled=True)  28 us
    all_gather x1, waiting for transfers between devices, on_device(): lax.all_gather(vit_out, 'dp', axis=0, tiled=True)  24.7 us
  transfers between devices with their start and end apart: 22, of which 22 were waited for; matrix products, arithmetic and copies ran while one was open for 7% of the time, Pallas kernels for 0%

profile of v1, /device:TPU:0, one launch (start us, length us, event | category | flops | bytes accessed | tf_op | source)
XLA Modules:
  0.0 524.9 jit_solution(5358705703779297928)
XLA Ops:
  7.2 0.7 all-gather.4.cloned.1.call-update
  8.0 0.7 all-gather.6.cloned.1.call-update
  8.7 1.5 fusion.43
  12.1 1.0 convert_reduce_fusion
  13.2 1.1 fusion.14
  14.3 62.8 %all-gather.4.cloned.1.call-done = bf16[1280,1920]{1,0:T(8,128)(2,1)} async-done(((bf16[640,1920]{1,0:T(8,128)(2,1)}), bf16[1280,1920]{1,0:T(8,128)(2,1)}) %all-gather.4.cloned.1.call-update) | async-done | bytes 4915216 | tf_op jit(solution)/shard_map/all_gather | solution.py:116
  77.1 3.5 convolution_convert_fusion.3
  81.9 24.7 %all-gather.6.cloned.1.call-done = bf16[640,1280]{1,0:T(8,128)(2,1)} async-done(((bf16[320,1280]{1,0:T(8,128)(2,1)}), bf16[640,1280]{1,0:T(8,128)(2,1)}) %all-gather.6.cloned.1.call-update) | async-done | bytes 1638416 | tf_op jit(solution)/shard_map/all_gather | solution.py:117
  106.6 1.9 fusion.57
  109.1 7.4 %collective-permute-done = bf16[16,5120]{1,0:T(8,128)(2,1)S(1)} collective-permute-done((bf16[16,5120]{1,0:T(8,128)(2,1)S(1)}, bf16[16,5120]{1,0:T(8,128)(2,1)S(1)}, u32[]{:S(2)}, u32[]{:S(2)}) %collective-permute-start) | collective-permute-done | bytes 163872 | tf_op jit(solution)/shard_map/ppermute | solution.py:130
  116.6 7.4 %collective-permute-done.1 = bf16[16,5120]{1,0:T(8,128)(2,1)S(1)} collective-permute-done((bf16[16,5120]{1,0:T(8,128)(2,1)S(1)}, bf16[16,5120]{1,0:T(8,128)(2,1)S(1)}, u32[]{:S(2)}, u32[]{:S(2)}) %collective-permute-start.1) | collective-permute-done | bytes 163872 | tf_op jit(solution)/shard_map/ppermute | solution.py:130
  124.0 7.4 %collective-permute-done.2 = bf16[16,5120]{1,0:T(8,128)(2,1)S(1)} collective-permute-done((bf16[16,5120]{1,0:T(8,128)(2,1)S(1)}, bf16[16,5120]{1,0:T(8,128)(2,1)S(1)}, u32[]{:S(2)}, u32[]{:S(2)}) %collective-permute-start.2) | collective-permute-done | bytes 163872 | tf_op jit(solution)/shard_map/ppermute | solution.py:130
  131.4 7.4 %collective-permute-done.3 = bf16[16,5120]{1,0:T(8,128)(2,1)S(1)} collective-permute-done((bf16[16,5120]{1,0:T(8,128)(2,1)S(1)}, bf16[16,5120]{1,0:T(8,128)(2,1)S(1)}, u32[]{:S(2)}, u32[]{:S(2)}) %collective-permute-start.3) | collective-permute-done | bytes 163872 | tf_op jit(solution)/shard_map/ppermute | solution.py:130
  138.9 7.4 %collective-permute-done.4 = bf16[16,5120]{1,0:T(8,128)(2,1)S(1)} collective-permute-done((bf16[16,5120]{1,0:T(8,128)(2,1)S(1)}, bf16[16,5120]{1,0:T(8,128)(2,1)S(1)}, u32[]{:S(2)}, u32[]{:S(2)}) %collective-permute-start.4) | collective-permute-done | bytes 163872 | tf_op jit(solution)/shard_map/ppermute | solution.py:130
  146.3 7.4 %collective-permute-done.5 = bf16[16,5120]{1,0:T(8,128)(2,1)S(1)} collective-permute-done((bf16[16,5120]{1,0:T(8,128)(2,1)S(1)}, bf16[16,5120]{1,0:T(8,128)(2,1)S(1)}, u32[]{:S(2)}, u32[]{:S(2)}) %collective-permute-start.5) | collective-permute-done | bytes 163872 | tf_op jit(solution)/shard_map/ppermute | solution.py:130
  153.8 7.4 %collective-permute-done.6 = bf16[16,5120]{1,0:T(8,128)(2,1)S(1)} collective-permute-done((bf16[16,5120]{1,0:T(8,128)(2,1)S(1)}, bf16[16,5120]{1,0:T(8,128)(2,1)S(1)}, u32[]{:S(2)}, u32[]{:S(2)}) %collective-permute-start.6) | collective-permute-done | bytes 163872 | tf_op jit(solution)/shard_map/ppermute | solution.py:130
  161.2 7.4 %collective-permute-done.7 = bf16[16,5120]{1,0:T(8,128)(2,1)S(1)} collective-permute-done((bf16[16,5120]{1,0:T(8,128)(2,1)S(1)}, bf16[16,5120]{1,0:T(8,128)(2,1)S(1)}, u32[]{:S(2)}, u32[]{:S(2)}) %collective-permute-start.7) | collective-permute-done | bytes 163872 | tf_op jit(solution)/shard_map/ppermute | solution.py:130
  168.6 7.4 %collective-permute-done.8 = bf16[16,5120]{1,0:T(8,128)(2,1)S(1)} collective-permute-done((bf16[16,5120]{1,0:T(8,128)(2,1)S(1)}, bf16[16,5120]{1,0:T(8,128)(2,1)S(1)}, u32[]{:S(2)}, u32[]{:S(2)}) %collective-permute-start.8) | collective-permute-done | bytes 163872 | tf_op jit(solution)/shard_map/ppermute | solution.py:130
  176.1 7.4 %collective-permute-done.9 = bf16[16,5120]{1,0:T(8,128)(2,1)S(1)} collective-permute-done((bf16[16,5120]{1,0:T(8,128)(2,1)S(1)}, bf16[16,5120]{1,0:T(8,128)(2,1)S(1)}, u32[]{:S(2)}, u32[]{:S(2)}) %collective-permute-start.9) | collective-permute-done | bytes 163872 | tf_op jit(solution)/shard_map/ppermute | solution.py:130
  183.5 7.4 %collective-permute-done.10 = bf16[16,5120]{1,0:T(8,128)(2,1)S(1)} collective-permute-done((bf16[16,5120]{1,0:T(8,128)(2,1)S(1)}, bf16[16,5120]{1,0:T(8,128)(2,1)S(1)}, u32[]{:S(2)}, u32[]{:S(2)}) %collective-permute-start.10) | collective-permute-done | bytes 163872 | tf_op jit(solution)/shard_map/ppermute | solution.py:130
  191.0 7.4 %collective-permute-done.11 = bf16[16,5120]{1,0:T(8,128)(2,1)S(1)} collective-permute-done((bf16[16,5120]{1,0:T(8,128)(2,1)S(1)}, bf16[16,5120]{1,0:T(8,128)(2,1)S(1)}, u32[]{:S(2)}, u32[]{:S(2)}) %collective-permute-start.11) | collective-permute-done | bytes 163872 | tf_op jit(solution)/shard_map/ppermute | solution.py:130
  198.4 7.4 %collective-permute-done.12 = bf16[16,5120]{1,0:T(8,128)(2,1)S(1)} collective-permute-done((bf16[16,5120]{1,0:T(8,128)(2,1)S(1)}, bf16[16,5120]{1,0:T(8,128)(2,1)S(1)}, u32[]{:S(2)}, u32[]{:S(2)}) %collective-permute-start.12) | collective-permute-done | bytes 163872 | tf_op jit(solution)/shard_map/ppermute | solution.py:130
  205.9 7.4 %collective-permute-done.13 = bf16[16,5120]{1,0:T(8,128)(2,1)S(1)} collective-permute-done((bf16[16,5120]{1,0:T(8,128)(2,1)S(1)}, bf16[16,5120]{1,0:T(8,128)(2,1)S(1)}, u32[]{:S(2)}, u32[]{:S(2)}) %collective-permute-start.13) | collective-permute-done | bytes 163872 | tf_op jit(solution)/shard_map/ppermute | solution.py:130
  213.3 7.4 %collective-permute-done.14 = bf16[16,5120]{1,0:T(8,128)(2,1)S(1)} collective-permute-done((bf16[16,5120]{1,0:T(8,128)(2,1)S(1)}, bf16[16,5120]{1,0:T(8,128)(2,1)S(1)}, u32[]{:S(2)}, u32[]{:S(2)}) %collective-permute-start.14) | collective-permute-done | bytes 163872 | tf_op jit(solution)/shard_map/ppermute | solution.py:130
  220.7 0.7 constant_dynamic-update-slice_fusion.31
  221.4 0.7 constant_dynamic-update-slice_fusion.30
  222.1 0.7 constant_dynamic-update-slice_fusion.29
  222.8 0.7 constant_dynamic-update-slice_fusion.28
  223.4 0.7 constant_dynamic-update-slice_fusion.27
  224.1 0.7 constant_dynamic-update-slice_fusion.26
  224.8 0.7 constant_dynamic-update-slice_fusion.25
  225.5 0.7 constant_dynamic-update-slice_fusion.24
  226.2 0.7 constant_dynamic-update-slice_fusion.23
  226.8 0.7 constant_dynamic-update-slice_fusion.22
  229.5 0.7 constant_dynamic-update-slice_fusion.18
  230.9 0.8 constant_dynamic-update-slice_fusion.16
  238.4 0.7 constant_dynamic-update-slice_fusion.5
  241.8 0.8 constant_dynamic-update-slice_fusion
  242.6 32.2 %all-gather.8.cloned.1.call-done = bf16[5120,512]{1,0:T(8,128)(2,1)} async-done(((bf16[2560,512]{1,0:T(8,128)(2,1)}), bf16[5120,512]{1,0:T(8,128)(2,1)}) %all-gather.8.cloned.1.call-update) | async-done | bytes 5242896 | tf_op jit(solution)/shard_map/all_gather | solution.py:118
  274.8 4.8 fusion.5
  280.0 0.8 copy.48
  280.8 5.6 %all-to-all-start = ((bf16[16,16,512]{2,1,0:T(8,128)(2,1)}), bf16[16,16,512]{2,1,0:T(8,128)(2,1)S(1)}, u32[]{:S(2)}, u32[]{:S(2)}) async-start(bf16[16,16,512]{2,1,0:T(8,128)(2,1)} %copy.48), calls=%async_computation | async-start | bytes 524288 | tf_op jit(solution)/shard_map/all_to_all | solution.py:145
  289.8 1.3 fusion.45
  291.1 1.5 add_select_fusion.1
  292.6 3.9 all-to-all-done
  296.5 0.9 multiply_reduce_fusion
  298.1 28.0 %all_to_all.65 = bf16[128,2,4096]{2,0,1:T(8,128)(2,1)S(1)} all-to-all(bf16[128,2,4096]{2,0,1:T(8,128)(2,1)S(1)} %bitcast.111), channel_id=1, replica_groups=mesh['dp'=2,'ctx'=16] {'dp'}, dimensions={1} | all-to-all | bytes 4194304 | tf_op jit(solution)/shard_map/all_to_all | solution.py:164
  326.1 2.0 convolution_convert_fusion.5
  328.6 9.1 %reduce-scatter.3.cloned.1.call-done = bf16[128,512]{1,0:T(8,128)(2,1)} async-done(((bf16[256,512]{1,0:T(8,128)(2,1)}), bf16[128,512]{1,0:T(8,128)(2,1)}) %reduce-scatter.3.cloned.1.call-update) | async-done | bytes 131088 | tf_op jit(solution)/shard_map/reduce_scatter | solution.py:165
  337.7 1.0 reshape.495
  339.6 4.4 all_gather.15
  344.0 4.2 convolution_convert_fusion.2
  348.2 3.4 all-to-all-start.2
  352.2 4.7 all-to-all-done.2
  358.7 6.7 %copy.53 = bf16[1,16,8192]{1,0,2:T(2,128)(2,1)} copy(bf16[1,16,8192]{2,1,0:T(8,128)(2,1)S(1)} %select_convert_fusion) | data formatting | bytes 524288 | tf_op jit(solution)/shard_map/convert_element_type | solution.py:197
  365.9 45.2 %reduce.3 = bf16[8192,16]{1,0:T(8,128)(2,1)S(1)} reduce(bf16[8192,1,16]{2,1,0:T(2,128)(2,1)} %bitcast.108, bf16[]{:T(256)} %broadcast.491), dimensions={1}, to_apply=%bitcast.90.reduce_sub_computation | reduce | bytes 524290
  411.2 2.1 reshape.502
  413.3 15.4 %all_to_all.66 = bf16[16,2,4096]{2,1,0:T(2,128)(2,1)S(1)} all-to-all(bf16[16,2,4096]{2,1,0:T(2,128)(2,1)S(1)} %reshape.502), channel_id=1, replica_groups=mesh['dp'=2,'ctx'=16] {'ctx'}, dimensions={0} | all-to-all | bytes 524288 | tf_op jit(solution)/shard_map/all_to_all | solution.py:198
  428.8 7.6 %reshape.503 = bf16[8192,1,16]{2,1,0:T(2,128)(2,1)} reshape(bf16[16,2,4096]{2,1,0:T(2,128)(2,1)S(1)} %all_to_all.66) | data formatting | bytes 524288
  436.3 7.9 %copy.54 = bf16[1,16,8192]{2,1,0:T(8,128)(2,1)S(1)} copy(bf16[1,16,8192]{1,0,2:T(2,128)(2,1)} %bitcast.109) | data formatting | bytes 524288 | tf_op jit(solution)/shard_map/all_to_all | solution.py:198
  444.7 5.6 %convolution_convert_fusion.1 = bf16[5120,512]{1,0:T(8,128)(2,1)} fusion(bf16[256,512]{1,0:T(8,128)(2,1)S(1)} %bitcast.116, bf16[512,5120]{1,0:T(8,128)(2,1)} %constant_dynamic-update-slice_fusion, s32[]{:T(128)S(6)} %select_n.126), kind=kOutput, calls=%fused_computation.3 | convolution fusion | flops 1344798720 | bytes 8126468 | tf_op jit(solution)/shard_map/dot_general | solution.py:204
  450.6 0.7 convert_element_type.180
  451.3 62.3 %reduce-scatter.5.cloned.1.call-done = bf16[2560,512]{1,0:T(8,128)(2,1)} async-done(((bf16[5120,512]{1,0:T(8,128)(2,1)}), bf16[2560,512]{1,0:T(8,128)(2,1)}) %reduce-scatter.5.cloned.1.call-update) | async-done | bytes 2621456 | tf_op jit(solution)/shard_map/reduce_scatter | solution.py:203
  513.5 4.8 convert_element_type.196
  (102 shorter events, 22.0 us)
Async XLA Ops:
  7.2 69.9 %all-gather.4.cloned.1.call-start = ((), (), s32[]{:S(2)}) async-start(), calls=%async_computation.6 | async-start | bytes 7372800 | tf_op jit(solution)/shard_map/all_gather | solution.py:116
  7.9 98.7 %copy-start.1 = (bf16[1,64,1280]{2,1,0:T(8,128)(2,1)S(1)}, bf16[1,64,1280]{2,1,0:T(8,128)(2,1)}, u32[]{:S(2)}) copy-start(bf16[1,64,1280]{2,1,0:T(8,128)(2,1)} %param.11) | copy-start | bytes 491524
  7.9 98.7 %all-gather.6.cloned.1.call-start = ((), (), s32[]{:S(2)}) async-start(), calls=%async_computation.7 | async-start | bytes 2457600 | tf_op jit(solution)/shard_map/all_gather | solution.py:117
  8.7 266.2 %all-gather.8.cloned.1.call-start = ((), (), s32[]{:S(2)}) async-start(), calls=%async_computation.8 | async-start | bytes 7864320 | tf_op jit(solution)/shard_map/all_gather | solution.py:118
  80.6 132.7 %copy-start.5 = (s32[1,16]{1,0:T(1,128)S(1)}, s32[1,16]{1,0:T(1,128)}, u32[]{:S(2)}) copy-start(s32[1,16]{1,0:T(1,128)} %param.21) | copy-start | bytes 196
  109.1 7.5 %collective-permute-start = (bf16[16,5120]{1,0:T(8,128)(2,1)S(1)}, bf16[16,5120]{1,0:T(8,128)(2,1)S(1)}, u32[]{:S(2)}, u32[]{:S(2)}) collective-permute-start(bf16[16,5120]{1,0:T(8,128)(2,1)S(1)} %broadcast_select_fusion), channel_id=1, source_target_pairs={{0,1},{1,2},{2,3},{3,4},{4,5},{5,6},{6,7},{7,8},{8,9},{9,10},{10,1... | collective-permute-start | bytes 491528 | tf_op jit(solution)/shard_map/ppermute | solution.py:130
  116.6 7.4 %collective-permute-start.1 = (bf16[16,5120]{1,0:T(8,128)(2,1)S(1)}, bf16[16,5120]{1,0:T(8,128)(2,1)S(1)}, u32[]{:S(2)}, u32[]{:S(2)}) collective-permute-start(bf16[16,5120]{1,0:T(8,128)(2,1)S(1)} %collective-permute-done), channel_id=1, source_target_pairs={{0,1},{1,2},{2,3},{3,4},{4,5},{5,6},{6,7},{7,8},{8,9},{9,10},{10,1... | collective-permute-start | bytes 491528 | tf_op jit(solution)/shard_map/ppermute | solution.py:130
  124.0 7.4 %collective-permute-start.2 = (bf16[16,5120]{1,0:T(8,128)(2,1)S(1)}, bf16[16,5120]{1,0:T(8,128)(2,1)S(1)}, u32[]{:S(2)}, u32[]{:S(2)}) collective-permute-start(bf16[16,5120]{1,0:T(8,128)(2,1)S(1)} %collective-permute-done.1), channel_id=1, source_target_pairs={{0,1},{1,2},{2,3},{3,4},{4,5},{5,6},{6,7},{7,8},{8,9},{9,10},{10,1... | collective-permute-start | bytes 491528 | tf_op jit(solution)/shard_map/ppermute | solution.py:130
  131.4 7.4 %collective-permute-start.3 = (bf16[16,5120]{1,0:T(8,128)(2,1)S(1)}, bf16[16,5120]{1,0:T(8,128)(2,1)S(1)}, u32[]{:S(2)}, u32[]{:S(2)}) collective-permute-start(bf16[16,5120]{1,0:T(8,128)(2,1)S(1)} %collective-permute-done.2), channel_id=1, source_target_pairs={{0,1},{1,2},{2,3},{3,4},{4,5},{5,6},{6,7},{7,8},{8,9},{9,10},{10,1... | collective-permute-start | bytes 491528 | tf_op jit(solution)/shard_map/ppermute | solution.py:130
  138.9 7.4 %collective-permute-start.4 = (bf16[16,5120]{1,0:T(8,128)(2,1)S(1)}, bf16[16,5120]{1,0:T(8,128)(2,1)S(1)}, u32[]{:S(2)}, u32[]{:S(2)}) collective-permute-start(bf16[16,5120]{1,0:T(8,128)(2,1)S(1)} %collective-permute-done.3), channel_id=1, source_target_pairs={{0,1},{1,2},{2,3},{3,4},{4,5},{5,6},{6,7},{7,8},{8,9},{9,10},{10,1... | collective-permute-start | bytes 491528 | tf_op jit(solution)/shard_map/ppermute | solution.py:130
  146.3 7.4 %collective-permute-start.5 = (bf16[16,5120]{1,0:T(8,128)(2,1)S(1)}, bf16[16,5120]{1,0:T(8,128)(2,1)S(1)}, u32[]{:S(2)}, u32[]{:S(2)}) collective-permute-start(bf16[16,5120]{1,0:T(8,128)(2,1)S(1)} %collective-permute-done.4), channel_id=1, source_target_pairs={{0,1},{1,2},{2,3},{3,4},{4,5},{5,6},{6,7},{7,8},{8,9},{9,10},{10,1... | collective-permute-start | bytes 491528 | tf_op jit(solution)/shard_map/ppermute | solution.py:130
  153.8 7.4 %collective-permute-start.6 = (bf16[16,5120]{1,0:T(8,128)(2,1)S(1)}, bf16[16,5120]{1,0:T(8,128)(2,1)S(1)}, u32[]{:S(2)}, u32[]{:S(2)}) collective-permute-start(bf16[16,5120]{1,0:T(8,128)(2,1)S(1)} %collective-permute-done.5), channel_id=1, source_target_pairs={{0,1},{1,2},{2,3},{3,4},{4,5},{5,6},{6,7},{7,8},{8,9},{9,10},{10,1... | collective-permute-start | bytes 491528 | tf_op jit(solution)/shard_map/ppermute | solution.py:130
  161.2 7.4 %collective-permute-start.7 = (bf16[16,5120]{1,0:T(8,128)(2,1)S(1)}, bf16[16,5120]{1,0:T(8,128)(2,1)S(1)}, u32[]{:S(2)}, u32[]{:S(2)}) collective-permute-start(bf16[16,5120]{1,0:T(8,128)(2,1)S(1)} %collective-permute-done.6), channel_id=1, source_target_pairs={{0,1},{1,2},{2,3},{3,4},{4,5},{5,6},{6,7},{7,8},{8,9},{9,10},{10,1... | collective-permute-start | bytes 491528 | tf_op jit(solution)/shard_map/ppermute | solution.py:130
  168.6 7.4 %collective-permute-start.8 = (bf16[16,5120]{1,0:T(8,128)(2,1)S(1)}, bf16[16,5120]{1,0:T(8,128)(2,1)S(1)}, u32[]{:S(2)}, u32[]{:S(2)}) collective-permute-start(bf16[16,5120]{1,0:T(8,128)(2,1)S(1)} %collective-permute-done.7), channel_id=1, source_target_pairs={{0,1},{1,2},{2,3},{3,4},{4,5},{5,6},{6,7},{7,8},{8,9},{9,10},{10,1... | collective-permute-start | bytes 491528 | tf_op jit(solution)/shard_map/ppermute | solution.py:130
  176.1 7.4 %collective-permute-start.9 = (bf16[16,5120]{1,0:T(8,128)(2,1)S(1)}, bf16[16,5120]{1,0:T(8,128)(2,1)S(1)}, u32[]{:S(2)}, u32[]{:S(2)}) collective-permute-start(bf16[16,5120]{1,0:T(8,128)(2,1)S(1)} %collective-permute-done.8), channel_id=1, source_target_pairs={{0,1},{1,2},{2,3},{3,4},{4,5},{5,6},{6,7},{7,8},{8,9},{9,10},{10,1... | collective-permute-start | bytes 491528 | tf_op jit(solution)/shard_map/ppermute | solution.py:130
  183.5 7.4 %collective-permute-start.10 = (bf16[16,5120]{1,0:T(8,128)(2,1)S(1)}, bf16[16,5120]{1,0:T(8,128)(2,1)S(1)}, u32[]{:S(2)}, u32[]{:S(2)}) collective-permute-start(bf16[16,5120]{1,0:T(8,128)(2,1)S(1)} %collective-permute-done.9), channel_id=1, source_target_pairs={{0,1},{1,2},{2,3},{3,4},{4,5},{5,6},{6,7},{7,8},{8,9},{9,10},{10,1... | collective-permute-start | bytes 491528 | tf_op jit(solution)/shard_map/ppermute | solution.py:130
  191.0 7.4 %collective-permute-start.11 = (bf16[16,5120]{1,0:T(8,128)(2,1)S(1)}, bf16[16,5120]{1,0:T(8,128)(2,1)S(1)}, u32[]{:S(2)}, u32[]{:S(2)}) collective-permute-start(bf16[16,5120]{1,0:T(8,128)(2,1)S(1)} %collective-permute-done.10), channel_id=1, source_target_pairs={{0,1},{1,2},{2,3},{3,4},{4,5},{5,6},{6,7},{7,8},{8,9},{9,10},{10,1... | collective-permute-start | bytes 491528 | tf_op jit(solution)/shard_map/ppermute | solution.py:130
  198.4 7.4 %collective-permute-start.12 = (bf16[16,5120]{1,0:T(8,128)(2,1)S(1)}, bf16[16,5120]{1,0:T(8,128)(2,1)S(1)}, u32[]{:S(2)}, u32[]{:S(2)}) collective-permute-start(bf16[16,5120]{1,0:T(8,128)(2,1)S(1)} %collective-permute-done.11), channel_id=1, source_target_pairs={{0,1},{1,2},{2,3},{3,4},{4,5},{5,6},{6,7},{7,8},{8,9},{9,10},{10,1... | collective-permute-start | bytes 491528 | tf_op jit(solution)/shard_map/ppermute | solution.py:130
  205.8 7.4 %collective-permute-start.13 = (bf16[16,5120]{1,0:T(8,128)(2,1)S(1)}, bf16[16,5120]{1,0:T(8,128)(2,1)S(1)}, u32[]{:S(2)}, u32[]{:S(2)}) collective-permute-start(bf16[16,5120]{1,0:T(8,128)(2,1)S(1)} %collective-permute-done.12), channel_id=1, source_target_pairs={{0,1},{1,2},{2,3},{3,4},{4,5},{5,6},{6,7},{7,8},{8,9},{9,10},{10,1... | collective-permute-start | bytes 491528 | tf_op jit(solution)/shard_map/ppermute | solution.py:130
  213.3 7.4 %collective-permute-start.14 = (bf16[16,5120]{1,0:T(8,128)(2,1)S(1)}, bf16[16,5120]{1,0:T(8,128)(2,1)S(1)}, u32[]{:S(2)}, u32[]{:S(2)}) collective-permute-start(bf16[16,5120]{1,0:T(8,128)(2,1)S(1)} %collective-permute-done.13), channel_id=1, source_target_pairs={{0,1},{1,2},{2,3},{3,4},{4,5},{5,6},{6,7},{7,8},{8,9},{9,10},{10,1... | collective-permute-start | bytes 491528 | tf_op jit(solution)/shard_map/ppermute | solution.py:130
  242.6 53.9 %copy-start.2 = (bf16[1,128,8192]{2,1,0:T(8,128)(2,1)S(1)}, bf16[1,128,8192]{2,1,0:T(8,128)(2,1)}, u32[]{:S(2)}) copy-start(bf16[1,128,8192]{2,1,0:T(8,128)(2,1)} %param.16) | copy-start | bytes 6291460
  279.6 17.8 %copy-start.3 = (f32[8192]{0:T(1024)S(1)}, f32[8192]{0:T(1024)}, u32[]{:S(2)}) copy-start(f32[8192]{0:T(1024)} %param.17) | copy-start | bytes 98308
  280.8 15.6 %all-to-all-start = ((bf16[16,16,512]{2,1,0:T(8,128)(2,1)}), bf16[16,16,512]{2,1,0:T(8,128)(2,1)S(1)}, u32[]{:S(2)}, u32[]{:S(2)}) async-start(bf16[16,16,512]{2,1,0:T(8,128)(2,1)} %copy.48), calls=%async_computation | async-start | bytes 524288 | tf_op jit(solution)/shard_map/all_to_all | solution.py:145
  286.5 51.2 %reduce-scatter.3.cloned.1.call-start = ((), (), s32[]{:S(2)}) async-start(), calls=%async_computation.9 | async-start | bytes 393216 | tf_op jit(solution)/shard_map/reduce_scatter | solution.py:165
  297.9 28.2 %copy-start = (bf16[4096,512]{1,0:T(8,128)(2,1)S(1)}, bf16[4096,512]{1,0:T(8,128)(2,1)}, u32[]{:S(2)}) copy-start(bf16[4096,512]{1,0:T(8,128)(2,1)} %param.18) | copy-start | bytes 12582916
  298.1 30.1 %copy-start.4 = (bf16[1,128,512]{2,1,0:T(8,128)(2,1)S(1)}, bf16[1,128,512]{2,1,0:T(8,128)(2,1)}, u32[]{:S(2)}) copy-start(bf16[1,128,512]{2,1,0:T(8,128)(2,1)} %param.19) | copy-start | bytes 393220
  348.2 8.6 %all-to-all-start.2 = ((bf16[2,16,4096]{2,1,0:T(8,128)(2,1)}), bf16[2,16,4096]{2,1,0:T(8,128)(2,1)S(1)}, u32[]{:S(2)}, u32[]{:S(2)}) async-start(bf16[2,16,4096]{2,1,0:T(8,128)(2,1)} %bitcast.17), calls=%async_computation.3 | async-start | bytes 524288 | tf_op jit(solution)/shard_map/all_to_all | solution.py:193
  351.7 161.9 %reduce-scatter.5.cloned.1.call-start = ((), (), s32[]{:S(2)}) async-start(), calls=%async_computation.10 | async-start | bytes 7864320 | tf_op jit(solution)/shard_map/reduce_scatter | solution.py:203
Sparse Core Ops, SparseCore 0:
  9.5 67.5 all-gather.3
  78.6 27.9 all-gather.5
  206.0 68.7 all-gather.7
  328.2 9.3 reduce-scatter.2
  450.5 63.0 reduce-scatter.4
